TPU v7x, 32 devices: a whole 2x2x4 slice. The times are simulated.
32 devices in a mesh: dp: 8 (over z, x), tensor: 4 (over y, core).
Axes of the slice: x: 2, y: 2, z: 4, core: 2. Of those that a mesh axis runs over, the one named last changes fastest.
Arguments:
- layer_input: bfloat16 [8192, 2048], P('dp'), may hold values from -6 to 6
- ln1_gain: bfloat16 [2048], replicated, may hold values from 0.099609375 to 1.8984375
- ln1_bias: bfloat16 [2048], replicated, may hold values from -3 to 3
- ln2_gain: bfloat16 [2048], replicated, may hold values from 0.099609375 to 1.8984375
- ln2_bias: bfloat16 [2048], replicated, may hold values from -3 to 3
- qkv_weight: bfloat16 [2048, 6144], P(None, 'tensor'), may hold values from -0.125 to 0.125
- qkv_bias: bfloat16 [6144], P('tensor'), may hold values from -1.75 to 1.75
- dense_weight: bfloat16 [2048, 2048], P(None, 'tensor'), may hold values from -0.75 to 0.75
- dense_bias: bfloat16 [2048], replicated, may hold values from -3 to 3
- fc1_weight: bfloat16 [2048, 8192], P(None, 'tensor'), may hold values from -0.125 to 0.125
- fc1_bias: bfloat16 [8192], P('tensor'), may hold values from -3 to 3
- fc2_weight: bfloat16 [2048, 8192], P(None, 'tensor'), may hold values from -0.0625 to 0.0625
- fc2_bias: bfloat16 [2048], replicated, may hold values from -3 to 3
- cotangent: bfloat16 [8192, 2048], P('dp'), may hold values from -6 to 6
Outputs:
- output: bfloat16 [8192, 2048], P('dp')
- input_grad: bfloat16 [8192, 2048], P('dp')
- grad_ln1_gain: float32 [2048], replicated
- grad_ln1_bias: float32 [2048], replicated
- grad_ln2_gain: float32 [2048], replicated
- grad_ln2_bias: float32 [2048], replicated
- grad_qkv_weight: float32 [2048, 6144], P('dp', 'tensor')
- grad_qkv_bias: float32 [6144], P('tensor')
- grad_dense_weight: float32 [2048, 2048], P('dp', 'tensor')
- grad_dense_bias: float32 [2048], replicated
- grad_fc1_weight: float32 [2048, 8192], P('dp', 'tensor')
- grad_fc1_bias: float32 [8192], P('tensor')
- grad_fc2_weight: float32 [2048, 8192], P('dp', 'tensor')
- grad_fc2_bias: float32 [2048], replicated
All inputs are finite; a program needn't handle non-finite values.
Results may differ from a plain program's by a relative error of at most 0.013.
Values may be sent and summed in bfloat16 or wider, within the bound.
A program may use at most 256 MiB of HBM per device.

v0:
```python
from functools import partial
import math

import jax
import jax.numpy as jnp
from jax import lax
from jax.sharding import PartitionSpec as P

HEADS = 8
SEQ = 1024
HEAD_DIM = 256
ROT = 64


EPSILON = 1e-05


def normalize(x_float, gain_row, shift_row):
    row_mean = jnp.mean(x_float, -1, keepdims=True)
    centred = x_float - row_mean
    spread = jnp.mean(centred * centred, -1, keepdims=True)
    return centred * lax.rsqrt(spread + EPSILON) * gain_row + shift_row


def rotary_tables():
    half_rot = ROT // 2
    freq_index = jnp.arange(half_rot, dtype=jnp.float32)
    frequency = jnp.exp(freq_index * (-2.0 * math.log(10000.0) / ROT))
    angles = jnp.arange(SEQ, dtype=jnp.float32)[:, None] * frequency[None, :]
    return (jnp.cos(angles), jnp.sin(angles))


def rotate(operand, cos_table, sine_table):
    half_rot = ROT // 2
    first_half = operand[..., :half_rot]
    second_half = operand[..., half_rot:ROT]
    cos_part = cos_table[None, :, None, :]
    sine_part = sine_table[None, :, None, :]
    return jnp.concatenate(
        [
            first_half * cos_part - second_half * sine_part,
            second_half * cos_part + first_half * sine_part,
            operand[..., ROT:],
        ],
        -1,
    )


def unrotate(operand, cos_table, sine_table):
    half_rot = ROT // 2
    first_half = operand[..., :half_rot]
    second_half = operand[..., half_rot:ROT]
    cos_part = cos_table[None, :, None, :]
    sine_part = sine_table[None, :, None, :]
    return jnp.concatenate(
        [
            first_half * cos_part + second_half * sine_part,
            second_half * cos_part - first_half * sine_part,
            operand[..., ROT:],
        ],
        -1,
    )


def block_scores(query_block, key_block, start_row, score_scale):
    scores = (
        jnp.einsum("sqhd,skhd->shqk", query_block, key_block, preferred_element_type=jnp.float32)
        * score_scale
    )
    row_ids = start_row + jnp.arange(query_block.shape[1])[:, None]
    col_ids = jnp.arange(key_block.shape[1])[None, :]
    return jnp.where(col_ids <= row_ids, scores, -1e30)


def rounded(values_in):
    return lax.optimization_barrier(values_in.astype(jnp.bfloat16)).astype(jnp.float32)


def on_device(
    layer_input,
    ln1_gain,
    ln1_bias,
    ln2_gain,
    ln2_bias,
    qkv_weight,
    qkv_bias,
    dense_weight,
    dense_bias,
    fc1_weight,
    fc1_bias,
    fc2_weight,
    fc2_bias,
    cotangent,
):
    tok_rows, model_width = layer_input.shape
    local_heads = HEADS // lax.axis_size("tensor")
    seq_count = tok_rows // SEQ
    block_rows = 512
    score_scale = HEAD_DIM ** (-0.5)
    x_float = layer_input.astype(jnp.float32)
    gain_one = ln1_gain.astype(jnp.float32)
    shift_one = ln1_bias.astype(jnp.float32)
    gain_two = ln2_gain.astype(jnp.float32)
    shift_two = ln2_bias.astype(jnp.float32)
    attn_in = normalize(x_float, gain_one, shift_one).astype(jnp.bfloat16)
    mlp_in = normalize(x_float, gain_two, shift_two).astype(jnp.bfloat16)
    qkv_all = jnp.dot(attn_in, qkv_weight, preferred_element_type=jnp.float32) + qkv_bias.astype(
        jnp.float32
    )
    qkv_all = qkv_all.reshape(seq_count, SEQ, local_heads, 3, HEAD_DIM)
    cos_table, sine_table = rotary_tables()
    queries = rotate(qkv_all[..., 0, :], cos_table, sine_table).astype(jnp.bfloat16)
    keys_rot = rotate(qkv_all[..., 1, :], cos_table, sine_table).astype(jnp.bfloat16)
    values = qkv_all[..., 2, :].astype(jnp.bfloat16)
    context_blocks = []
    log_sums = []
    for start_row in range(0, SEQ, block_rows):
        key_end = start_row + block_rows
        masked = block_scores(
            queries[:, start_row:key_end], keys_rot[:, :key_end], start_row, score_scale
        )
        row_peak = jnp.max(masked, -1, keepdims=True)
        weights = jnp.exp(masked - row_peak)
        row_total = jnp.sum(weights, -1, keepdims=True)
        probabilities = (weights / row_total).astype(jnp.bfloat16)
        log_sums.append(row_peak + jnp.log(row_total))
        context_blocks.append(
            jnp.einsum(
                "shqk,skhd->sqhd",
                probabilities,
                values[:, :key_end],
                preferred_element_type=jnp.float32,
            )
        )
    context = jnp.concatenate(context_blocks, 1).astype(jnp.bfloat16)
    context_flat = context.reshape(tok_rows, local_heads * HEAD_DIM)
    attn_part = jnp.einsum(
        "td,ed->te", context_flat, dense_weight, preferred_element_type=jnp.float32
    )
    hidden = jnp.dot(mlp_in, fc1_weight, preferred_element_type=jnp.float32) + fc1_bias.astype(
        jnp.float32
    )
    exact_gelu = partial(jax.nn.gelu, approximate=False)
    activated = exact_gelu(hidden).astype(jnp.bfloat16)
    mlp_part = jnp.einsum("tf,ef->te", activated, fc2_weight, preferred_element_type=jnp.float32)
    partial_out = attn_part + mlp_part
    bias_total = dense_bias.astype(jnp.float32) + fc2_bias.astype(jnp.float32)
    full_sum = lax.psum(partial_out, "tensor")
    output = (x_float + full_sum + bias_total).astype(jnp.bfloat16)
    out_grad = cotangent.astype(jnp.float32)
    grad_fc2 = jnp.einsum("te,tf->ef", cotangent, activated, preferred_element_type=jnp.float32)
    grad_dense = jnp.einsum(
        "te,td->ed", cotangent, context_flat, preferred_element_type=jnp.float32
    )
    out_bias_grad = jnp.sum(out_grad, 0)
    activated_grad = jnp.einsum(
        "te,ef->tf", cotangent, fc2_weight, preferred_element_type=jnp.float32
    )
    gelu_pull = jax.vjp(exact_gelu, hidden)[1]
    hidden_grad = gelu_pull(activated_grad)[0].astype(jnp.bfloat16)
    grad_fc1 = jnp.einsum("td,tf->df", mlp_in, hidden_grad, preferred_element_type=jnp.float32)
    fc1_bias_grad = jnp.sum(hidden_grad.astype(jnp.float32), 0)
    mlp_in_grad = jnp.einsum(
        "tf,df->td", hidden_grad, fc1_weight, preferred_element_type=jnp.float32
    )
    context_grad = jnp.einsum(
        "te,ed->td", cotangent, dense_weight, preferred_element_type=jnp.float32
    ).astype(jnp.bfloat16)
    context_grad = context_grad.reshape(seq_count, SEQ, local_heads, HEAD_DIM)
    key_grad = jnp.zeros((seq_count, SEQ, local_heads, HEAD_DIM), jnp.float32)
    value_grad = jnp.zeros((seq_count, SEQ, local_heads, HEAD_DIM), jnp.float32)
    query_grads = []
    for block_number, start_row in enumerate(range(0, SEQ, block_rows)):
        key_end = start_row + block_rows
        query_block = queries[:, start_row:key_end]
        masked = block_scores(query_block, keys_rot[:, :key_end], start_row, score_scale)
        probabilities = jnp.exp(masked - log_sums[block_number])
        grad_block = context_grad[:, start_row:key_end]
        value_grad = value_grad.at[:, :key_end].add(
            jnp.einsum(
                "shqk,sqhd->skhd",
                probabilities.astype(jnp.bfloat16),
                grad_block,
                preferred_element_type=jnp.float32,
            )
        )
        prob_grad = jnp.einsum(
            "sqhd,skhd->shqk", grad_block, values[:, :key_end], preferred_element_type=jnp.float32
        )
        row_delta = jnp.sum(probabilities * prob_grad, -1, keepdims=True)
        score_grad = (probabilities * (prob_grad - row_delta)).astype(jnp.bfloat16)
        query_grads.append(
            jnp.einsum(
                "shqk,skhd->sqhd",
                score_grad,
                keys_rot[:, :key_end],
                preferred_element_type=jnp.float32,
            )
            * score_scale
        )
        key_grad = key_grad.at[:, :key_end].add(
            jnp.einsum(
                "shqk,sqhd->skhd", score_grad, query_block, preferred_element_type=jnp.float32
            )
            * score_scale
        )
    query_grad = jnp.concatenate(query_grads, 1)
    query_pre = unrotate(rounded(query_grad), cos_table, sine_table).astype(jnp.bfloat16)
    key_pre = unrotate(rounded(key_grad), cos_table, sine_table).astype(jnp.bfloat16)
    value_pre = value_grad.astype(jnp.bfloat16)
    qkv_grad = jnp.stack([query_pre, key_pre, value_pre], 3).reshape(
        tok_rows, local_heads * 3 * HEAD_DIM
    )
    grad_qkv = jnp.einsum("td,tc->dc", attn_in, qkv_grad, preferred_element_type=jnp.float32)
    qkv_bias_grad = jnp.sum(qkv_grad.astype(jnp.float32), 0)
    attn_in_grad = jnp.einsum("tc,dc->td", qkv_grad, qkv_weight, preferred_element_type=jnp.float32)
    norm_one_pull = jax.vjp(normalize, x_float, gain_one, shift_one)[1]
    input_one, gain_grad_one, shift_grad_one = norm_one_pull(attn_in_grad)
    norm_two_pull = jax.vjp(normalize, x_float, gain_two, shift_two)[1]
    input_two, gain_grad_two, shift_grad_two = norm_two_pull(mlp_in_grad)
    input_part = input_one + input_two
    input_total = lax.psum(input_part, "tensor")
    input_grad = (out_grad + input_total).astype(jnp.bfloat16)
    qkv_bias_grad, fc1_bias_grad, out_bias_grad = lax.psum(
        (qkv_bias_grad, fc1_bias_grad, out_bias_grad), "dp"
    )
    gain_grad_one, shift_grad_one, gain_grad_two, shift_grad_two = lax.psum(
        (gain_grad_one, shift_grad_one, gain_grad_two, shift_grad_two), ("dp", "tensor")
    )
    grad_qkv, grad_dense, grad_fc1, grad_fc2 = (
        lax.psum_scatter(
            grad_qkv.astype(jnp.bfloat16), "dp", scatter_dimension=0, tiled=True
        ).astype(jnp.float32),
        lax.psum_scatter(
            grad_dense.astype(jnp.bfloat16), "dp", scatter_dimension=0, tiled=True
        ).astype(jnp.float32),
        lax.psum_scatter(
            grad_fc1.astype(jnp.bfloat16), "dp", scatter_dimension=0, tiled=True
        ).astype(jnp.float32),
        lax.psum_scatter(
            grad_fc2.astype(jnp.bfloat16), "dp", scatter_dimension=0, tiled=True
        ).astype(jnp.float32),
    )
    return (
        output,
        input_grad,
        gain_grad_one,
        shift_grad_one,
        gain_grad_two,
        shift_grad_two,
        grad_qkv,
        qkv_bias_grad,
        grad_dense,
        out_bias_grad,
        grad_fc1,
        fc1_bias_grad,
        grad_fc2,
        out_bias_grad,
    )


def solution(mesh):
    in_specs = (
        P("dp", None),
        P(),
        P(),
        P(),
        P(),
        P(None, "tensor"),
        P("tensor"),
        P(None, "tensor"),
        P(),
        P(None, "tensor"),
        P("tensor"),
        P(None, "tensor"),
        P(),
        P("dp", None),
    )
    out_specs = (
        P("dp", None),
        P("dp", None),
        P(),
        P(),
        P(),
        P(),
        P("dp", "tensor"),
        P("tensor"),
        P("dp", "tensor"),
        P(),
        P("dp", "tensor"),
        P("tensor"),
        P("dp", "tensor"),
        P(),
    )
    return jax.shard_map(
        on_device, mesh=mesh, in_specs=in_specs, out_specs=out_specs, check_vma=False
    )
```

profile of v0, /device:TPU:0, one launch (start us, length us, event | category | flops | bytes accessed | tf_op | source)
XLA Modules:
  0.0 675.3 jit_solution(8149849624211081454)
XLA Ops:
  8.2 3.0 convert_reduce_fusion
  13.6 11.6 %convolution_add_fusion = f32[1024,1536]{1,0:T(8,128)} fusion(bf16[2048,1536]{1,0:T(8,128)(2,1)} %param.31, f32[1536]{0:T(1024)S(1)} %convert_element_type.224, bf16[1024,2048]{1,0:T(8,128)(2,1)S(1)} %copy-done.1, f32[2048]{0:T(1024)S(1)} %convert_element_type.222, f32[2048]{0:T(1024)S(1)} %convert_element_type.221, f32[1024]{0:T(1024)S(1)} %fusion.64, ...), kind=kOutput, calls=%fused_computation.52 | convolution fusion | flops 6456606720 | bytes 16807936 | tf_op jit(solution)/shard_map/dot_general | solution.py:107
  25.1 6.6 copy.80
  34.5 4.8 fusion.80
  39.3 2.9 copy.128
  42.2 2.9 slice_bitcast_fusion.16
  45.1 2.9 slice.264
  51.1 3.4 copy.127
  56.6 3.2 subtract_convert_fusion.2
  64.0 3.1 fusion.48
  70.9 3.7 fusion.30
  74.9 4.7 convolution_convert_fusion.3
  95.2 3.9 pad_maximum_fusion.1
  99.1 4.7 copy.104
  103.8 12.8 %fusion.71 = f32[1024,2048]{1,0:T(8,128)S(1)} fusion(bf16[2048,2048]{1,0:T(8,128)(2,1)} %param.35, bf16[1024,2048]{1,0:T(8,128)(2,1)} %param.26, f32[2048]{0:T(1024)S(1)} %convert_element_type.231, f32[2048]{0:T(1024)S(1)} %convert_element_type.230, f32[1024]{0:T(1024)S(1)} %fusion.64, f32[1024]{0:T(1024)S(1)} %broadcast_multiply_fusion), kind=kOutput, calls=%fused_computation.152 | convolution fusion | flops 8602517504 | bytes 20996096 | tf_op jit(solution)/shard_map/dot_general | solution.py:140
  116.6 33.9 %convert_reduce_fusion.2 = (f32[2048]{0:T(1024)}, bf16[1024,2048]{1,0:T(8,128)(2,1)}, f32[1024,2048]{1,0:T(8,128)}) fusion(f32[1024,2048]{1,0:T(8,128)S(1)} %fusion.71, f32[2048]{0:T(1024)S(1)} %convert_element_type.233, bf16[1024,2048]{1,0:T(8,128)(2,1)S(1)} %copy-done.18, bf16[2048,2048]{1,0:T(8,128)(2,1)} %param.37), kind=kOutput, calls=%fused_computation.32 | convolution fusion | flops 8747218944 | bytes 33570816 | tf_op jit(solution)/shard_map/te,ef->tf/dot_general | solution.py:156
  150.5 10.0 %multiply_convert_fusion = bf16[1024,2048]{1,0:T(8,128)(2,1)} fusion(f32[1024,2048]{1,0:T(8,128)} %get-tuple-element.141, f32[1024,2048]{1,0:T(8,128)} %copy-done.10, f32[2048]{0:T(1024)S(1)} %convert_element_type.233), kind=kLoop, calls=%fused_computation.35 | loop fusion | flops 8388608 | bytes 20979712 | tf_op jit(solution)/shard_map/convert_element_type | solution.py:144
  160.5 12.7 %fusion.84 = f32[1024,2048]{1,0:T(8,128)S(1)} fusion(bf16[1024,2048]{1,0:T(8,128)(2,1)} %get-tuple-element.140, bf16[2048,2048]{1,0:T(8,128)(2,1)} %param.35), kind=kOutput, calls=%fused_computation.162 | convolution fusion | flops 8589934592 | bytes 20971520 | tf_op jit(solution)/shard_map/tf,df->td/dot_general | solution.py:163
  173.3 14.0 %fusion.78 = (f32[2048]{0:T(1024)}, f32[1024]{0:T(1024)}, f32[1024]{0:T(1024)}, f32[2048]{0:T(1024)}, f32[1024,2048]{1,0:T(8,128)}) fusion(f32[2048]{0:T(1024)S(1)} %copy-done.38, f32[1024]{0:T(1024)S(1)} %broadcast_multiply_fusion, bf16[1024,2048]{1,0:T(8,128)(2,1)S(1)} %copy-done.2, f32[1024,2048]{1,0:T(8,128)S(1)} %fusion.84, f32[2048]{0:T(1024)} %copy-done.39, ...), kind=kOutput, calls=%fused_computation.156 | convolution fusion | flops 6463416320 | bytes 30453760 | tf_op jit(solution)/shard_map/tc,dc->td/dot_general | solution.py:216
  188.0 9.2 %fusion.16 = (f32[2048]{0:T(1024)S(1)}, f32[1024]{0:T(1024)S(1)}, f32[1024]{0:T(1024)S(1)}, f32[2048]{0:T(1024)S(1)}) fusion(f32[1024,2048]{1,0:T(8,128)S(1)} %fusion.84, bf16[1024,2048]{1,0:T(8,128)(2,1)S(1)} %copy-done.2, f32[1024]{0:T(1024)} %copy-done.42, f32[1024]{0:T(1024)S(1)} %broadcast_multiply_fusion, f32[1024]{0:T(1024)S(1)} %get-tuple-element.165, ...), kind=kLoop, calls=%fused_computation.24 | loop fusion | flops 39839744 | bytes 21028864 | tf_op jit(solution)/shard_map/transpose(jvp())/reduce_sum | solution.py:22
  197.3 13.3 %fusion.83 = f32[1024,2048]{1,0:T(8,128)} fusion(bf16[1024,2048]{1,0:T(8,128)(2,1)S(1)} %copy-done.15, bf16[2048,2048]{1,0:T(8,128)(2,1)} %param.37), kind=kOutput, calls=%fused_computation.161 | convolution fusion | flops 8589934592 | bytes 20971520 | tf_op jit(solution)/shard_map/tf,ef->te/dot_general | solution.py:145
  210.6 9.1 %convolution_add_fusion.1 = f32[1024,2048]{1,0:T(8,128)} fusion(f32[1024,2048]{1,0:T(8,128)} %fusion.83, bf16[2048,512]{1,0:T(8,128)(2,1)S(1)} %copy-done, bf16[512,512]{0,1:T(8,128)(2,1)S(1)} %bitcast.186, bf16[512,512]{0,1:T(8,128)(2,1)S(1)} %bitcast.188), kind=kOutput, calls=%fused_computation.59 | convolution fusion | flops 2151677952 | bytes 19922944 | tf_op jit(solution)/shard_map/td,ed->te/dot_general | solution.py:137
  219.8 6.7 add_add_fusion.2
  227.2 13.8 %convolution_convert_fusion.1 = bf16[2048,1536]{1,0:T(8,128)(2,1)} fusion(bf16[1024,1536]{0,1:T(8,128)(2,1)} %bitcast.179, bf16[1024,2048]{1,0:T(8,128)(2,1)} %param.26, f32[2048]{0:T(1024)S(1)} %copy-done.46, f32[2048]{0:T(1024)S(1)} %copy-done.38, f32[1024]{0:T(1024)S(1)} %copy-done.43, f32[1024]{0:T(1024)S(1)} %broadcast_multiply_fusion), kind=kOutput, calls=%fused_computation.50 | convolution fusion | flops 6458179584 | bytes 13656064 | tf_op jit(solution)/shard_map/td,tc->dc/dot_general | solution.py:214
  241.7 14.7 %convolution_convert_fusion = bf16[2048,2048]{1,0:T(8,128)(2,1)} fusion(bf16[1024,2048]{1,0:T(8,128)(2,1)} %get-tuple-element.140, bf16[1024,2048]{1,0:T(8,128)(2,1)} %param.26, f32[2048]{0:T(1024)S(1)} %copy-done.48, f32[2048]{0:T(1024)S(1)} %copy-done.40, f32[1024]{0:T(1024)S(1)} %copy-done.43, f32[1024]{0:T(1024)S(1)} %broadcast_multiply_fusion), kind=kOutput, calls=%fused_computation.49 | convolution fusion | flops 8606711808 | bytes 16801792 | tf_op jit(solution)/shard_map/td,tf->df/dot_general | solution.py:161
  256.4 14.4 %convert_bitcast_fusion = bf16[2048,2048]{0,1:T(8,128)(2,1)} fusion(bf16[1024,2048]{1,0:T(8,128)(2,1)} %multiply_convert_fusion, bf16[1024,2048]{1,0:T(8,128)(2,1)} %param.39), kind=kOutput, calls=%fused_computation.31 | convolution fusion | flops 8594128896 | bytes 16777216 | tf_op jit(solution)/shard_map/te,tf->ef/dot_general | solution.py:151
  276.6 45.7 %all-reduce.2 = (f32[2048]{0:T(1024)}, f32[2048]{0:T(1024)}, f32[2048]{0:T(1024)}, f32[2048]{0:T(1024)}) all-reduce(f32[2048]{0:T(1024)S(1)} %get-tuple-element.129, f32[2048]{0:T(1024)S(1)} %copy-done.50, f32[2048]{0:T(1024)S(1)} %get-tuple-element.120, f32[2048]{0:T(1024)S(1)} %copy-done.51), channel_id=1, replica_groups=mesh['dp'=8,'tensor'=4] {'dp','tensor'}, use_global_device_ids=true, to_apply=%region_15.16 | all-reduce | flops 8192 | bytes 65536 | tf_op jit(solution)/shard_map/psum | solution.py:227
  324.2 194.7 %all-reduce.7.cloned.1.call-done = (f32[1024,2048]{1,0:T(8,128)}, f32[1024,2048]{1,0:T(8,128)}) async-done(((f32[1024,2048]{1,0:T(8,128)}, f32[1024,2048]{1,0:T(8,128)}), (f32[1024,2048]{1,0:T(8,128)}, f32[1024,2048]{1,0:T(8,128)})) %all-reduce.7.cloned.1.call-update) | async-done | bytes 16777232 | tf_op jit(solution)/shard_map/psum | solution.py:148
  518.9 9.2 %convert_reduce_fusion.1 = (f32[2048]{0:T(1024)S(1)}, bf16[1024,2048]{1,0:T(8,128)(2,1)}) fusion(bf16[1024,2048]{1,0:T(8,128)(2,1)} %param.39, f32[1024,2048]{1,0:T(8,128)} %get-tuple-element.138), kind=kLoop, calls=%fused_computation.16 | loop fusion | flops 8386560 | bytes 16785408 | tf_op jit(solution)/shard_map/reduce_sum | solution.py:155
  528.2 40.2 %all-reduce.3 = (f32[1536]{0:T(1024)}, f32[2048]{0:T(1024)S(1)}, f32[2048]{0:T(1024)}) all-reduce(f32[1536]{0:T(1024)S(1)} %reduce_sum.177, f32[2048]{0:T(1024)S(1)} %get-tuple-element.146, f32[2048]{0:T(1024)S(1)} %copy-done.44), channel_id=1, replica_groups=mesh['dp'=8,'tensor'=4] {'dp'}, use_global_device_ids=true, to_apply=%region_24.25 | all-reduce | flops 5632 | bytes 45056 | tf_op jit(solution)/shard_map/psum | solution.py:224
  568.4 8.4 %fusion.21 = bf16[1024,2048]{1,0:T(8,128)(2,1)} fusion(f32[1024,2048]{1,0:T(8,128)} %get-tuple-element.137, bf16[1024,2048]{1,0:T(8,128)(2,1)} %param.26, f32[2048]{0:T(1024)S(1)} %convert_add_fusion.2), kind=kLoop, calls=%fused_computation.29 | loop fusion | flops 8388608 | bytes 16785408 | tf_op jit(solution)/shard_map/convert_element_type | solution.py:149
  582.1 82.4 %reduce-scatter.11.cloned.1.call-done = bf16[256,2048]{0,1:T(8,128)(2,1)} async-done(((bf16[2048,2048]{0,1:T(8,128)(2,1)}), bf16[256,2048]{0,1:T(8,128)(2,1)}) %reduce-scatter.11.cloned.1.call-update) | async-done | bytes 1048592 | tf_op jit(solution)/shard_map/reduce_scatter | solution.py:240
  (187 shorter events, 51.9 us)
Async XLA Ops:
  8.0 66.9 %copy-start = (bf16[2048,512]{1,0:T(8,128)(2,1)S(1)}, bf16[2048,512]{1,0:T(8,128)(2,1)}, u32[]{:S(2)}) copy-start(bf16[2048,512]{1,0:T(8,128)(2,1)} %param.33) | copy-start | bytes 6291460
  8.1 314.2 %reduce-scatter.7.cloned.1.call-start = ((), (), s32[]{:S(2)}) async-start(), calls=%async_computation.5 | async-start | bytes 2359296 | tf_op jit(solution)/shard_map/reduce_scatter | solution.py:234
  12.9 12.2 %copy-start.41 = (f32[1024]{0:T(1024)}, f32[1024]{0:T(1024)S(1)}, u32[]{:S(2)}) copy-start(f32[1024]{0:T(1024)S(1)} %fusion.17) | copy-start | bytes 12292
  13.0 90.8 %copy-start.42 = (f32[1024]{0:T(1024)}, f32[1024]{0:T(1024)S(1)}, u32[]{:S(2)}) copy-start(f32[1024]{0:T(1024)S(1)} %fusion.64) | copy-start | bytes 12292
  13.0 12.1 %copy-start.45 = (f32[2048]{0:T(1024)}, f32[2048]{0:T(1024)S(1)}, u32[]{:S(2)}) copy-start(f32[2048]{0:T(1024)S(1)} %convert_element_type.222) | copy-start | bytes 24580
  54.5 5.3 copy-start.16
  60.3 6.8 %copy-start.28 = (bf16[512,2,256]{2,0,1:T(8,128)(2,1)}, bf16[512,2,256]{2,0,1:T(8,128)(2,1)S(1)}, u32[]{:S(2)}) copy-start(bf16[512,2,256]{2,0,1:T(8,128)(2,1)S(1)} %fusion.56) | copy-start | bytes 1572868
  61.3 5.9 copy-start.20
  74.6 444.3 %all-reduce.7.cloned.1.call-start = ((), (), s32[]{:S(2)}) async-start(), calls=%async_computation.8 | async-start | bytes 33554432 | tf_op jit(solution)/shard_map/psum | solution.py:148
  92.9 10.9 %copy-start.39 = (f32[2048]{0:T(1024)}, f32[2048]{0:T(1024)S(1)}, u32[]{:S(2)}) copy-start(f32[2048]{0:T(1024)S(1)} %convert_element_type.230) | copy-start | bytes 24580
  92.9 10.9 %copy-start.47 = (f32[2048]{0:T(1024)}, f32[2048]{0:T(1024)S(1)}, u32[]{:S(2)}) copy-start(f32[2048]{0:T(1024)S(1)} %convert_element_type.231) | copy-start | bytes 24580
  103.8 12.8 %copy-start.18 = (bf16[1024,2048]{1,0:T(8,128)(2,1)S(1)}, bf16[1024,2048]{1,0:T(8,128)(2,1)}, u32[]{:S(2)}) copy-start(bf16[1024,2048]{1,0:T(8,128)(2,1)} %param.39) | copy-start | bytes 12582916
  116.6 33.9 %copy-start.10 = (f32[1024,2048]{1,0:T(8,128)}, f32[1024,2048]{1,0:T(8,128)S(1)}, u32[]{:S(2)}) copy-start(f32[1024,2048]{1,0:T(8,128)S(1)} %fusion.71) | copy-start | bytes 25165828
  160.5 12.7 %copy-start.2 = (bf16[1024,2048]{1,0:T(8,128)(2,1)S(1)}, bf16[1024,2048]{1,0:T(8,128)(2,1)}, u32[]{:S(2)}) copy-start(bf16[1024,2048]{1,0:T(8,128)(2,1)} %param.26) | copy-start | bytes 12582916
  160.5 12.7 %copy-start.19 = (bf16[1,1024,2,3,256]{1,4,3,2,0:T(8,128)(2,1)S(1)}, bf16[1,1024,2,3,256]{1,4,3,2,0:T(8,128)(2,1)}, u32[]{:S(2)}) copy-start(bf16[1,1024,2,3,256]{1,4,3,2,0:T(8,128)(2,1)} %copy.104) | copy-start | bytes 9437188
  160.5 12.7 %copy-start.38 = (f32[2048]{0:T(1024)S(1)}, f32[2048]{0:T(1024)}, u32[]{:S(2)}) copy-start(f32[2048]{0:T(1024)} %copy-done.37) | copy-start | bytes 24580
  188.0 9.2 %copy-start.15 = (bf16[1024,2048]{1,0:T(8,128)(2,1)S(1)}, bf16[1024,2048]{1,0:T(8,128)(2,1)}, u32[]{:S(2)}) copy-start(bf16[1024,2048]{1,0:T(8,128)(2,1)} %multiply_convert_fusion) | copy-start | bytes 12582916
  197.3 13.4 %copy-start.33 = (bf16[2,256,512]{2,1,0:T(8,128)(2,1)S(1)}, bf16[2,256,512]{2,1,0:T(8,128)(2,1)}, u32[]{:S(2)}) copy-start(bf16[2,256,512]{2,1,0:T(8,128)(2,1)} %copy-done.32) | copy-start | bytes 1572868
  197.3 13.3 %copy-start.35 = (bf16[2,256,512]{2,1,0:T(8,128)(2,1)S(1)}, bf16[2,256,512]{2,1,0:T(8,128)(2,1)}, u32[]{:S(2)}) copy-start(bf16[2,256,512]{2,1,0:T(8,128)(2,1)} %copy-done.34) | copy-start | bytes 1572868
  210.6 9.2 %copy-start.5 = (f32[1024,2048]{1,0:T(8,128)S(1)}, f32[1024,2048]{1,0:T(8,128)}, u32[]{:S(2)}) copy-start(f32[1024,2048]{1,0:T(8,128)} %get-tuple-element.176) | copy-start | bytes 25165828
  210.6 9.2 %copy-start.40 = (f32[2048]{0:T(1024)S(1)}, f32[2048]{0:T(1024)}, u32[]{:S(2)}) copy-start(f32[2048]{0:T(1024)} %copy-done.39) | copy-start | bytes 24580
  210.6 9.2 %copy-start.43 = (f32[1024]{0:T(1024)S(1)}, f32[1024]{0:T(1024)}, u32[]{:S(2)}) copy-start(f32[1024]{0:T(1024)} %copy-done.42) | copy-start | bytes 12292
  226.6 350.3 %reduce-scatter.5.cloned.1.call-start = ((), (), s32[]{:S(2)}) async-start(), calls=%async_computation.4 | async-start | bytes 7077888 | tf_op jit(solution)/shard_map/reduce_scatter | solution.py:231
  241.0 338.3 %reduce-scatter.9.cloned.1.call-start = ((), (), s32[]{:S(2)}) async-start(), calls=%async_computation.6 | async-start | bytes 9437184 | tf_op jit(solution)/shard_map/reduce_scatter | solution.py:237
  256.4 408.1 %reduce-scatter.11.cloned.1.call-start = ((), (), s32[]{:S(2)}) async-start(), calls=%async_computation.7 | async-start | bytes 9437184 | tf_op jit(solution)/shard_map/reduce_scatter | solution.py:240
  270.9 5.2 copy-start.9
  270.9 5.7 copy-start.50
  270.9 5.7 copy-start.51
  270.9 51.3 %copy-start.58 = (bf16[2048]{0:T(1024)(128)(2,1)S(1)}, bf16[2048]{0:T(1024)(128)(2,1)}, u32[]{:S(2)}) copy-start(bf16[2048]{0:T(1024)(128)(2,1)} %param.38) | copy-start | bytes 12292
  270.9 51.3 %copy-start.59 = (bf16[2048]{0:T(1024)(128)(2,1)S(1)}, bf16[2048]{0:T(1024)(128)(2,1)}, u32[]{:S(2)}) copy-start(bf16[2048]{0:T(1024)(128)(2,1)} %param.34) | copy-start | bytes 12292
  518.9 9.3 %copy-start.44 = (f32[2048]{0:T(1024)S(1)}, f32[2048]{0:T(1024)}, u32[]{:S(2)}) copy-start(f32[2048]{0:T(1024)} %get-tuple-element.139) | copy-start | bytes 24580
  568.4 98.6 %copy-start.49 = (f32[2048]{0:T(1024)}, f32[2048]{0:T(1024)S(1)}, u32[]{:S(2)}) copy-start(f32[2048]{0:T(1024)S(1)} %get-tuple-element.206) | copy-start | bytes 24580
  (33 other events, 96.4 us)
Sparse Core Ops, SparseCore 0:
  74.7 71.6 reduce-scatter.6
  241.2 121.7 reduce-scatter.4
  366.6 146.6 reduce-scatter.8
  516.8 147.6 reduce-scatter.10
Sparse Core Ops, SparseCore 1:
  226.6 292.2 all-reduce.6
where the time goes:
time: 683 us; the launch traced here: 675 us
  waiting for transfers between devices  277 us (41%)
  matrix products  173 us (25%)
  blocking collectives  85.9 us (13%)
  other arithmetic  75 us (11%)
  local copies, waits for them, and re-layouts  47.2 us (7%)
  between operations  16.7 us (2%)
    psum x1, waiting for transfers between devices, on_device(): full_sum = lax.psum(partial_out, 'tensor')  195 us
    reduce_scatter x1, waiting for transfers between devices, on_device(): lax.psum_scatter(grad_fc2.astype(jnp.bfloat16), 'dp', scatter_dimension=0...  82.4 us
    psum x1, blocking collectives, on_device(): lax.psum((gain_grad_one, shift_grad_one, gain_grad_two, shift_grad_two),...  45.7 us
    psum x1, blocking collectives, on_device(): lax.psum((qkv_bias_grad, fc1_bias_grad, out_bias_grad), 'dp')  40.2 us
    dot_general x1, matrix products, on_device(): jnp.einsum('te,ef->tf', cotangent, fc2_weight, preferred_element_type=jnp...  33.9 us
    unnamed x125, local copies, waits for them, and re-layouts  18.3 us
    dot_general x1, matrix products, on_device(): jnp.einsum('td,tf->df', mlp_in, hidden_grad, preferred_element_type=jnp.f...  14.7 us
    dot_general x1, matrix products, on_device(): jnp.einsum('te,tf->ef', cotangent, activated, preferred_element_type=jnp....  14.4 us
  transfers between devices with their start and end apart: 5, of which 2 were waited for; matrix products, arithmetic and copies ran while one was open for 33% of the time, Pallas kernels for 0%

commit v1 on v0

--- a/solution.py
+++ b/solution.py
@@ -1,18 +1,662 @@
+import itertools
+import math
 from functools import partial
-import math
 
 import jax
 import jax.numpy as jnp
 from jax import lax
+from jax.experimental import pallas as pl
+from jax.experimental.pallas import tpu as pltpu
 from jax.sharding import PartitionSpec as P
 
 HEADS = 8
 SEQ = 1024
 HEAD_DIM = 256
 ROT = 64
-
-
 EPSILON = 1e-05
+VMEM_LIMIT = 63 * 1024 * 1024
+
+f32 = jnp.float32
+bf16 = jnp.bfloat16
+NN = (((1,), (0,)), ((), ()))
+NT = (((1,), (1,)), ((), ()))
+TN = (((0,), (0,)), ((), ()))
+
+
+def dot(a, b, dims=NN):
+    return lax.dot_general(a, b, dims, preferred_element_type=f32)
+
+
+def turn(block, cos_table, sine_table):
+    half_rot = ROT // 2
+    head = block[:, :128]
+    lane = lax.broadcasted_iota(jnp.int32, head.shape, 1)
+    other = jnp.where(lane < half_rot, pltpu.roll(head, 128 - half_rot, 1), pltpu.roll(head, half_rot, 1))
+    return jnp.concatenate([head * cos_table + other * sine_table, block[:, 128:]], 1)
+
+
+def angle_tables():
+    half_rot = ROT // 2
+    lane = jnp.arange(128)
+    frequency = jnp.exp((lane % half_rot).astype(f32) * (-2.0 * math.log(10000.0) / ROT))
+    frequency = jnp.where(lane < ROT, frequency, 0.0)
+    step = jnp.arange(32, dtype=f32)
+    angles = jnp.concatenate([step, 32.0 * step])[:, None] * frequency[None, :]
+    cos, sin = jnp.cos(angles), jnp.sin(angles)
+    sign = jnp.where(lane < half_rot, -1.0, 1.0)[None, :]
+    return jnp.concatenate([cos[:32], sin[:32], cos[32:], sin[32:], jnp.broadcast_to(sign, (8, 128))], 0)
+
+
+CHUNK = 512
+MESH = pl.DeviceIdType.MESH
+VEC_ROWS = 8
+
+
+class Slots:
+    def __init__(self, count):
+        self.free = [(n, []) for n in range(count)]
+
+    def take(self):
+        slot, waits = self.free.pop(0)
+        for wait in waits:
+            wait()
+        return slot
+
+    def give(self, slot, *waits):
+        self.free.append((slot, list(waits)))
+
+    def drain(self):
+        for _, waits in self.free:
+            for wait in waits:
+                wait()
+
+
+def layer_kernel(
+    x_hbm, c_hbm, vec_in, table_in, fc1_hbm, fc2_hbm, wqkv_hbm, dense_hbm,
+    out_hbm, grad_hbm, keep_hbm, last_hbm, small_out, r1_hbm, r2_hbm, core_hbm, y_hbm,
+    attn_in, mlp_in, cot, act, hg, qg, ctx, mean_ref, rstd_ref, cos_ref, sin_ref, vec, w1buf, w2buf,
+    s1, s2, s3, k2, ld1, ldm, ld2, piece, xrow, small, small_in,
+    load_sem, weight_sem, send_sem, recv_sem, keep_sem,
+    *, jobs, orders, heads, block=256,
+):
+    rows, width = cot.shape
+    hidden = act.shape[1]
+    nb = width // 8
+    quarter = rows // 4
+    me, own = lax.axis_index("dp"), lax.axis_index("tensor")
+    dp_bits = [lax.rem(lax.div(me, 1 << k), 2) for k in range(3)]
+    t_bits = [lax.rem(lax.div(own, 1 << k), 2) for k in range(2)]
+
+    def dp_flip(*bits):
+        return me + sum((1 - 2 * dp_bits[k]) * (1 << k) for k in bits)
+
+    def t_flip(*bits):
+        return own + sum((1 - 2 * t_bits[k]) * (1 << k) for k in bits)
+
+    def dp_partner(bit):
+        return (dp_flip(bit), own)
+
+    def t_partner(bit):
+        return (me, t_flip(bit))
+
+    partners = [dp_partner(k) for k in range(3)] + [t_partner(k) for k in range(2)]
+    barrier = pltpu.get_barrier_semaphore()
+    for partner in partners:
+        pl.semaphore_signal(barrier, inc=1, device_id=partner, device_id_type=MESH)
+
+    copies = itertools.count()
+
+    def send_copy(src, dst, partner):
+        n = next(copies)
+        copy = pltpu.make_async_remote_copy(
+            src_ref=src, dst_ref=dst, send_sem=send_sem.at[n], recv_sem=recv_sem.at[n], device_id=partner, device_id_type=MESH
+        )
+        copy.start()
+        return copy
+
+    loads = itertools.count()
+
+    def load(src, dst):
+        copy = pltpu.make_async_copy(src, dst, load_sem.at[next(loads)])
+        copy.start()
+        return copy
+
+    load_x = load(x_hbm, act)
+    load_c = load(c_hbm, cot)
+
+    def mlp_weights(j):
+        slot = j % 2
+        at = pl.ds(j * CHUNK, CHUNK)
+        return [load(fc1_hbm.at[:, at], w1buf.at[slot]), load(fc2_hbm.at[:, at], w2buf.at[slot])]
+
+    def head_weights(h):
+        slot = h % 2
+        base = 3 * h * HEAD_DIM
+        return [
+            load(wqkv_hbm.at[:, pl.ds(base, 2 * HEAD_DIM)], w1buf.at[slot]),
+            load(wqkv_hbm.at[:, pl.ds(base + 2 * HEAD_DIM, HEAD_DIM)], w2buf.at[slot, :, pl.ds(0, HEAD_DIM)]),
+            load(dense_hbm.at[:, pl.ds(h * HEAD_DIM, HEAD_DIM)], w2buf.at[slot, :, pl.ds(HEAD_DIM, HEAD_DIM)]),
+        ]
+
+    weights = {("mlp", 0): mlp_weights(0), ("mlp", 1): mlp_weights(1)}
+    tiles = hidden // CHUNK
+
+    small[...] = jnp.zeros_like(small)
+    per_row = width // 128
+    for n in range(VEC_ROWS):
+        for i in range(per_row):
+            vec[n : n + 1, i * 128 : (i + 1) * 128] = vec_in[n * per_row + i : n * per_row + i + 1, :]
+    low_cos, low_sin = table_in[0:32, :], table_in[32:64, :]
+    sign = table_in[128:129, :]
+    for n in range(SEQ // 32):
+        high_cos, high_sin = table_in[64 + n : 65 + n, :], table_in[96 + n : 97 + n, :]
+        cos_ref[n * 32 : (n + 1) * 32, :] = high_cos * low_cos - high_sin * low_sin
+        sin_ref[n * 32 : (n + 1) * 32, :] = sign * (high_sin * low_cos + high_cos * low_sin)
+
+    load_x.wait()
+
+    def norm_rows(i, _):
+        part = pl.ds(pl.multiple_of(i * 128, 128), 128)
+        x = act[part, :].astype(f32)
+        mean = jnp.mean(x, -1, keepdims=True)
+        centred = x - mean
+        rstd = lax.rsqrt(jnp.mean(centred * centred, -1, keepdims=True) + EPSILON)
+        u = centred * rstd
+        attn_in[part, :] = (u * vec[0:1, :] + vec[1:2, :]).astype(bf16)
+        mlp_in[part, :] = (u * vec[2:3, :] + vec[3:4, :]).astype(bf16)
+        mean_ref[part, :] = mean
+        rstd_ref[part, :] = rstd
+        return 0
+
+    lax.fori_loop(0, rows // 128, norm_rows, 0)
+    load_c.wait()
+    pl.semaphore_wait(barrier, len(partners))
+
+    s1_slots, s2_slots, s3_slots, k2_slots = Slots(s1.shape[0]), Slots(s2.shape[0]), Slots(s3.shape[0]), Slots(k2.shape[0])
+    state = {}
+
+    def operands(c):
+        n_fc = hidden // CHUNK
+        n_qkv = qg.shape[1] // CHUNK
+        if c < n_fc:
+            return cot, act, c
+        if c < 2 * n_fc:
+            return mlp_in, hg, c - n_fc
+        if c < 2 * n_fc + n_qkv:
+            return attn_in, qg, c - 2 * n_fc
+        return cot, ctx, c - 2 * n_fc - n_qkv
+
+    def block_of(lhs, index):
+        return lhs[:, pl.ds(pl.multiple_of(index * nb, nb), nb)]
+
+    def w1(c):
+        lhs, rhs, j = operands(c)
+        one, two, three = orders[c]
+        slot = s1_slots.take()
+        base = dp_flip(one, two, three)
+
+        def body(n, _):
+            second, third = n // 2, lax.rem(n, 2)
+            index = base - second * (1 - 2 * dp_bits[two]) * (1 << two) - third * (1 - 2 * dp_bits[three]) * (1 << three)
+            s1[slot, n] = dot(block_of(lhs, index), rhs[:, j * CHUNK : (j + 1) * CHUNK], TN).astype(bf16)
+            return 0
+
+        lax.fori_loop(0, 4, body, 0)
+        copy = send_copy(s1.at[slot], r1_hbm.at[c], dp_partner(one))
+        s1_slots.give(slot, copy.wait_send)
+        state[c] = copy
+
+    def w2(c):
+        lhs, rhs, j = operands(c)
+        one, two, three = orders[c]
+        state[c].wait_recv()
+        loaded = load(r1_hbm.at[c], ld1)
+        slot, kept = s2_slots.take(), k2_slots.take()
+        loaded.wait()
+
+        def part(base, n, out):
+            def body(i, _):
+                index = base - i * (1 - 2 * dp_bits[three]) * (1 << three)
+                out[i] = (dot(block_of(lhs, index), rhs[:, j * CHUNK : (j + 1) * CHUNK], TN) + ld1[n + i].astype(f32)).astype(bf16)
+                return 0
+
+            lax.fori_loop(0, 2, body, 0)
+
+        part(dp_flip(two, three), 0, s2.at[slot])
+        copy = send_copy(s2.at[slot], r2_hbm.at[c], dp_partner(two))
+        s2_slots.give(slot, copy.wait_send)
+        part(dp_flip(three), 2, k2.at[kept])
+        state[c] = (copy, kept)
+
+    def a3(c):
+        copy, kept = state[c]
+        three = orders[c][2]
+        copy.wait_recv()
+        loaded = load(r2_hbm.at[c], ld2)
+        slot = s3_slots.take()
+        loaded.wait()
+        s3[slot] = (k2[kept, 0].astype(f32) + ld2[0].astype(f32)).astype(bf16)
+        columns = pl.ds(c * CHUNK, CHUNK)
+        copy = send_copy(s3.at[slot], last_hbm.at[:, columns], dp_partner(three))
+        s3_slots.give(slot, copy.wait_send)
+        k2[kept, 1] = (k2[kept, 1].astype(f32) + ld2[1].astype(f32)).astype(bf16)
+        keep = pltpu.make_async_copy(k2.at[kept, 1], keep_hbm.at[:, columns], keep_sem.at[c])
+        keep.start()
+        k2_slots.give(kept, keep.wait)
+        state[c] = copy
+
+    def mlp(j):
+        slot = j % 2
+        for copy in weights.pop(("mlp", j)):
+            copy.wait()
+        at = j * CHUNK
+        bias = vec[4:5, at : at + CHUNK]
+
+        def body(i, sums):
+            part = pl.ds(pl.multiple_of(i * block, block), block)
+            h = dot(mlp_in[part, :], w1buf[slot]) + bias
+            above = dot(cot[part, :], w2buf[slot])
+            cdf = 0.5 + 0.5 * lax.erf(h * (2.0**-0.5))
+            density = jnp.exp(h * h * -0.5) * ((2.0 * math.pi) ** -0.5)
+            act[part, at : at + CHUNK] = (h * cdf).astype(bf16)
+            low = (above * (cdf + h * density)).astype(bf16)
+            hg[part, at : at + CHUNK] = low
+            above_sum = jnp.sum(cot[part, at : at + CHUNK].astype(f32), 0, keepdims=True)
+            return sums[0] + jnp.sum(low.astype(f32), 0, keepdims=True), sums[1] + above_sum
+
+        zero = jnp.zeros((1, CHUNK), f32)
+        bias_sum, above_sum = lax.fori_loop(0, rows // block, body, (zero, zero))
+        small[4:5, at : at + CHUNK] = bias_sum
+        small[6:7, at : at + CHUNK] = above_sum
+        if j + 2 < tiles:
+            weights["mlp", j + 2] = mlp_weights(j + 2)
+        else:
+            h = j + 2 - tiles
+            weights["head", h] = head_weights(h)
+
+    def attention(h):
+        slot = h % 2
+        for copy in weights.pop(("head", h)):
+            copy.wait()
+        base = 3 * h * HEAD_DIM
+        scale = HEAD_DIM ** (-0.5)
+
+        def scoped(qkv_ref, g_ref, dk_ref, dv_ref):
+            def project(i, _):
+                part = pl.ds(pl.multiple_of(i * block, block), block)
+                acc = dot(attn_in[part, :], w1buf[slot]) + vec[7:8, base : base + 2 * HEAD_DIM]
+                cos, sin = cos_ref[part, :], sin_ref[part, :]
+                for n in range(2):
+                    at = n * HEAD_DIM
+                    qkv_ref[part, at : at + HEAD_DIM] = turn(acc[:, at : at + HEAD_DIM], cos, sin).astype(bf16)
+                acc = dot(attn_in[part, :], w2buf[slot, :, 0:HEAD_DIM]) + vec[7:8, base + 2 * HEAD_DIM : base + 3 * HEAD_DIM]
+                qkv_ref[part, 2 * HEAD_DIM :] = acc.astype(bf16)
+                g_ref[part, :] = dot(cot[part, :], w2buf[slot, :, HEAD_DIM : 2 * HEAD_DIM]).astype(bf16)
+                return 0
+
+            lax.fori_loop(0, rows // block, project, 0)
+            for i in reversed(range(SEQ // block)):
+                part = pl.ds(i * block, block)
+                key_end = (i + 1) * block
+                keys = pl.ds(0, key_end)
+                q, g = qkv_ref[part, 0:HEAD_DIM], g_ref[part, :]
+                k, v = qkv_ref[keys, HEAD_DIM : 2 * HEAD_DIM], qkv_ref[keys, 2 * HEAD_DIM :]
+                scores = dot(q, k, NT) * scale
+                row_id = i * block + lax.broadcasted_iota(jnp.int32, scores.shape, 0)
+                col_id = lax.broadcasted_iota(jnp.int32, scores.shape, 1)
+                scores = jnp.where(col_id <= row_id, scores, -1e30)
+                e = jnp.exp(scores - jnp.max(scores, -1, keepdims=True))
+                probs = e / jnp.sum(e, -1, keepdims=True)
+                low = probs.astype(bf16)
+                ctx[part, h * HEAD_DIM : (h + 1) * HEAD_DIM] = dot(low, v).astype(bf16)
+                prob_grad = dot(g, v, NT)
+                delta = jnp.sum(probs * prob_grad, -1, keepdims=True)
+                score_grad = (probs * (prob_grad - delta)).astype(bf16)
+                dv = dot(low, g, TN)
+                dk = dot(score_grad, q, TN)
+                if i == SEQ // block - 1:
+                    dv_ref[...] = dv
+                    dk_ref[...] = dk
+                else:
+                    dv_ref[keys, :] += dv
+                    dk_ref[keys, :] += dk
+                dq = (dot(score_grad, k) * scale).astype(bf16).astype(f32)
+                qg[part, base : base + HEAD_DIM] = turn(dq, cos_ref[part, :], -sin_ref[part, :]).astype(bf16)
+            dk = (dk_ref[...] * scale).astype(bf16).astype(f32)
+            qg[:, base + HEAD_DIM : base + 2 * HEAD_DIM] = turn(dk, cos_ref[...], -sin_ref[...]).astype(bf16)
+            qg[:, base + 2 * HEAD_DIM : base + 3 * HEAD_DIM] = dv_ref[...].astype(bf16)
+            head = qg[:, base : base + 3 * HEAD_DIM]
+            small[5:6, base : base + 3 * HEAD_DIM] = jnp.sum(head.astype(f32), 0, keepdims=True)
+
+        pl.run_scoped(
+            scoped,
+            pltpu.VMEM((SEQ, 3 * HEAD_DIM), bf16),
+            pltpu.VMEM((SEQ, HEAD_DIM), bf16),
+            pltpu.VMEM((SEQ, HEAD_DIM), f32),
+            pltpu.VMEM((SEQ, HEAD_DIM), f32),
+        )
+        if h + 2 < heads:
+            weights["head", h + 2] = head_weights(h + 2)
+
+    quarters = [t_flip(0, 1), t_flip(0), t_flip(1), own]
+
+    def quarter_of(n):
+        return pl.ds(pl.multiple_of(quarters[n] * quarter, quarter), quarter)
+
+    def back_tiles(buf, first_hbm, first, second_hbm, second, x_tiles, store):
+        step = CHUNK // 2
+
+        def scoped(first_w, second_w, x_w, sems):
+            def copies_of(d, slot):
+                at = pl.ds(pl.multiple_of(d * step, step), step)
+                made = [
+                    pltpu.make_async_copy(first_hbm.at[at, :], first_w.at[slot], sems.at[slot, 0]),
+                    pltpu.make_async_copy(second_hbm.at[at, :], second_w.at[slot], sems.at[slot, 1]),
+                ]
+                if x_tiles:
+                    made.append(pltpu.make_async_copy(x_hbm.at[:, at], x_w.at[slot], sems.at[slot, 2]))
+                return made
+
+            n_steps = width // step
+            for copy in copies_of(0, 0):
+                copy.start()
+
+            def body(e, _):
+                for half in range(2):
+                    d = 2 * e + half
+                    for copy in copies_of(d, half):
+                        copy.wait()
+
+                    @pl.when(d + 1 < n_steps)
+                    def _():
+                        for copy in copies_of(d + 1, 1 - half):
+                            copy.start()
+
+                    columns = pl.ds(half * step, step)
+                    sums = [jnp.zeros((1, step), f32) for _ in range(4)]
+                    for n in range(4):
+                        part = quarter_of(n)
+                        a = dot(first[part, :], first_w[half], NT)
+                        b = dot(second[part, :], second_w[half], NT)
+                        at = pl.ds(pl.multiple_of(e * 2 * quarter + (n % 2) * quarter, quarter), quarter)
+                        buf[n // 2, at, columns], terms = store(d, part, a, b, x_w.at[half])
+                        sums = [s + t for s, t in zip(sums, terms)]
+                    if x_tiles:
+                        at = pl.ds(pl.multiple_of(d * step, step), step)
+                        small[0:4, at] = jnp.concatenate(sums, 0)
+                return 0
+
+            lax.fori_loop(0, n_steps // 2, body, 0)
+
+        pl.run_scoped(
+            scoped,
+            pltpu.VMEM((2, step, first.shape[1]), bf16),
+            pltpu.VMEM((2, step, second.shape[1]), bf16),
+            pltpu.VMEM((2, rows if x_tiles else 16, step), bf16),
+            pltpu.SemaphoreType.DMA((2, 3)),
+        )
+
+    def input_tiles():
+        step = CHUNK // 2
+
+        def store(d, part, a, b, x_tile):
+            at = pl.ds(pl.multiple_of(d * step, step), step)
+            u = (x_tile[part, :].astype(f32) - mean_ref[part, :]) * rstd_ref[part, :]
+            terms = [jnp.sum(t, 0, keepdims=True) for t in (a * u, a, b * u, b)]
+            return (a * vec[0:1, at] + b * vec[2:3, at]).astype(bf16), terms
+
+        back_tiles(w1buf, wqkv_hbm, qg, fc1_hbm, hg, True, store)
+
+    def output_tiles():
+        back_tiles(w2buf, dense_hbm, ctx, fc2_hbm, act, False, lambda d, part, a, b, x_tile: ((a + b).astype(bf16), []))
+
+    e_tiles = width // CHUNK
+    buffers = (w1buf, w2buf)
+    results = (grad_hbm, out_hbm)
+
+    def sum_start(k):
+        (input_tiles, output_tiles)[k]()
+        state["sum", k] = send_copy(buffers[k].at[0], core_hbm.at[k], t_partner(0))
+
+    def half_of(k, half, dst):
+        return [
+            load(core_hbm.at[k, pl.ds(e * 2 * quarter + half * quarter, quarter), :], dst.at[e]) for e in range(e_tiles)
+        ]
+
+    def sum_middle(k):
+        first = state["sum", k]
+        first.wait_recv()
+        loaded = half_of(k, 0, ld1)
+        slot = s1_slots.take()
+        for copy in loaded:
+            copy.wait()
+        for e in range(e_tiles):
+            s1[slot, e] = (buffers[k][1, pl.ds(e * 2 * quarter, quarter), :].astype(f32) + ld1[e].astype(f32)).astype(bf16)
+        copy = send_copy(s1.at[slot], y_hbm.at[k], t_partner(1))
+        s1_slots.give(slot, copy.wait_send)
+        first.wait_send()
+        state["sum", k] = copy
+
+    own_rows = pl.ds(pl.multiple_of(own * quarter, quarter), quarter)
+
+    def rows_of(index):
+        return pl.ds(pl.multiple_of(index * quarter, quarter), quarter)
+
+    def sum_late(k):
+        x_load = load(x_hbm.at[own_rows, :], xrow)
+        half_loads = half_of(k, 1, ld1)
+        state["sum", k].wait_recv()
+        y_load = load(y_hbm.at[k], ldm)
+        for copy in half_loads + [x_load, y_load]:
+            copy.wait()
+        totals = [
+            buffers[k][1, pl.ds(e * 2 * quarter + quarter, quarter), :].astype(f32) + ld1[e].astype(f32) + ldm[e].astype(f32)
+            for e in range(e_tiles)
+        ]
+        parts = [(e * CHUNK, (e + 1) * CHUNK) for e in range(e_tiles)]
+        if k == 0:
+            mean, rstd = mean_ref[own_rows, :], rstd_ref[own_rows, :]
+            us = [(xrow[:, a:b].astype(f32) - mean) * rstd for a, b in parts]
+            mean_w = sum(jnp.sum(t, -1, keepdims=True) for t in totals) * (1.0 / width)
+            mean_wu = sum(jnp.sum(t * u, -1, keepdims=True) for t, u in zip(totals, us)) * (1.0 / width)
+            for (a, b), t, u in zip(parts, totals, us):
+                piece[k, :, a:b] = (cot[own_rows, a:b].astype(f32) + rstd * (t - mean_w - u * mean_wu)).astype(bf16)
+        else:
+            for (a, b), t in zip(parts, totals):
+                piece[k, :, a:b] = (xrow[:, a:b].astype(f32) + t + vec[5:6, a:b]).astype(bf16)
+        result = results[k]
+        state["pieces", k] = [
+            load(piece.at[k], result.at[own_rows, :]),
+            send_copy(piece.at[k], result.at[own_rows, :], t_partner(1)),
+            send_copy(piece.at[k], result.at[own_rows, :], t_partner(0)),
+        ]
+
+    def sum_gather(k):
+        result = results[k]
+        state["pieces", k][1].wait_recv()
+        at = rows_of(t_flip(1))
+        state["pieces", k].append(send_copy(result.at[at, :], result.at[at, :], t_partner(0)))
+
+    def small_round(n):
+        if n > 0:
+            copy = state["small"]
+            copy.wait()
+            if n <= 2:
+                small[0:4, :] += small_in[n - 1, 0:4, :]
+            else:
+                small[...] += small_in[n - 1]
+        if n < 5:
+            partner = t_partner(n) if n < 2 else dp_partner(n - 2)
+            state["small"] = send_copy(small, small_in.at[n], partner)
+        else:
+            state["small"] = load(small, small_out)
+
+    actions = dict(
+        m=mlp, h=attention, a=w1, b=w2, c=a3, i=lambda k: sum_start(k), j=sum_middle, k=sum_late, l=sum_gather, s=small_round
+    )
+    for kind, n in jobs:
+        actions[kind](n)
+
+    for c in range(len(orders)):
+        state[c].wait_recv()
+    for k in range(2):
+        local, first, second, third = state["pieces", k]
+        local.wait()
+        first.wait_send()
+        second.wait()
+        third.wait()
+        state["sum", k]
+    for slots in (s1_slots, s2_slots, s3_slots, k2_slots):
+        slots.drain()
+    state["small"].wait()
+
+
+ORDER = " ".join(
+    [
+        "m0 a0 a4 m1",
+        "m2 a6 a5 m3",
+        "b0 b4 h0 h1",
+        "a3 a9 b6 c0",
+        "c4 b5 i0 a2",
+        "b3 j0 c6 b9",
+        "s0 i1 a8 c5",
+        "k0 j1 c3 c9",
+        "b2 s1 s2 a11",
+        "s3 s4 s5 l0",
+        "b8 a1 c2 k1",
+        "b11 c8 a7 b1",
+        "l1 c11 a10 c1",
+        "b7 b10 c7 c10",
+    ]
+).split()
+Z_FIRST = (0, 6, 9)
+
+
+def layer_call(x, c, ln_vectors, biases, fc1, fc2, qkv_weight, dense):
+    rows, width = x.shape
+    hidden, qkv_columns, context_columns = fc1.shape[1], qkv_weight.shape[1], dense.shape[1]
+    heads = qkv_columns // (3 * HEAD_DIM)
+    total = 2 * hidden + qkv_columns + context_columns
+    chunks = total // CHUNK
+    fc1_bias, qkv_bias, dense_bias, fc2_bias = (b.astype(f32) for b in biases)
+    pad = jnp.zeros((width - qkv_columns,), f32)
+    vectors = jnp.concatenate(
+        [*(v.astype(f32) for v in ln_vectors), fc1_bias, dense_bias + fc2_bias, fc1_bias, qkv_bias, pad]
+    ).reshape(-1, 128)
+    jobs = [(word[0], int(word[1:])) for word in ORDER]
+    orders = [(1, 0, 2) if n in Z_FIRST else (0, 1, 2) for n in range(chunks)]
+    quarter, nb = rows // 4, width // 8
+    anywhere = pl.BlockSpec(memory_space=pl.ANY)
+    local = pl.BlockSpec(memory_space=pltpu.VMEM)
+    shape = jax.ShapeDtypeStruct
+    outs = [
+        shape((rows, width), bf16),
+        shape((rows, width), bf16),
+        shape((nb, total), bf16),
+        shape((nb, total), bf16),
+        shape((8, width), f32),
+        shape((chunks, 4, nb, CHUNK), bf16),
+        shape((chunks, 2, nb, CHUNK), bf16),
+        shape((2, width // CHUNK * 2 * quarter, CHUNK), bf16),
+        shape((2, width // CHUNK, quarter, CHUNK), bf16),
+    ]
+    vmem = pltpu.VMEM
+    scratch = [
+        vmem((rows, width), bf16),
+        vmem((rows, width), bf16),
+        vmem((rows, width), bf16),
+        vmem((rows, hidden), bf16),
+        vmem((rows, hidden), bf16),
+        vmem((rows, qkv_columns), bf16),
+        vmem((rows, context_columns), bf16),
+        vmem((rows, 1), f32),
+        vmem((rows, 1), f32),
+        vmem((SEQ, 128), f32),
+        vmem((SEQ, 128), f32),
+        vmem((VEC_ROWS, width), f32),
+        vmem((2, width, CHUNK), bf16),
+        vmem((2, width, CHUNK), bf16),
+        vmem((4, 4, nb, CHUNK), bf16),
+        vmem((3, 2, nb, CHUNK), bf16),
+        vmem((3, nb, CHUNK), bf16),
+        vmem((6, 2, nb, CHUNK), bf16),
+        vmem((4, nb, CHUNK), bf16),
+        vmem((4, nb, CHUNK), bf16),
+        vmem((2, nb, CHUNK), bf16),
+        vmem((2, quarter, width), bf16),
+        vmem((quarter, width), bf16),
+        vmem((8, width), f32),
+        vmem((5, 8, width), f32),
+        pltpu.SemaphoreType.DMA((80,)),
+        pltpu.SemaphoreType.DMA((1,)),
+        pltpu.SemaphoreType.DMA((56,)),
+        pltpu.SemaphoreType.DMA((56,)),
+        pltpu.SemaphoreType.DMA((chunks,)),
+    ]
+    flops = 6 * rows * width * (2 * hidden + qkv_columns + context_columns)
+    return pl.pallas_call(
+        partial(layer_kernel, jobs=jobs, orders=orders, heads=heads),
+        in_specs=[anywhere, anywhere, local, local] + [anywhere] * 4,
+        out_specs=[anywhere] * len(outs),
+        out_shape=outs,
+        scratch_shapes=scratch,
+        compiler_params=pltpu.CompilerParams(vmem_limit_bytes=VMEM_LIMIT, collective_id=0, has_side_effects=True),
+        cost_estimate=pl.CostEstimate(flops=flops, bytes_accessed=1 << 27, transcendentals=2 * rows * hidden),
+        name="layer",
+    )(x, c, vectors, angle_tables(), fc1, fc2, qkv_weight, dense)
+
+
+def fused(
+    layer_input,
+    ln1_gain,
+    ln1_bias,
+    ln2_gain,
+    ln2_bias,
+    qkv_weight,
+    qkv_bias,
+    dense_weight,
+    dense_bias,
+    fc1_weight,
+    fc1_bias,
+    fc2_weight,
+    fc2_bias,
+    cotangent,
+):
+    output, input_grad, kept, last, small, *_ = layer_call(
+        layer_input,
+        cotangent,
+        (ln1_gain, ln1_bias, ln2_gain, ln2_bias),
+        (fc1_bias, qkv_bias, dense_bias, fc2_bias),
+        fc1_weight,
+        fc2_weight,
+        qkv_weight,
+        dense_weight,
+    )
+    hidden, qkv_columns = fc1_weight.shape[1], qkv_weight.shape[1]
+    ends = (0, hidden, 2 * hidden, 2 * hidden + qkv_columns, kept.shape[1])
+    grad_fc2, grad_fc1, grad_qkv, grad_dense = (
+        kept[:, a:b].astype(f32) + last[:, a:b].astype(f32) for a, b in zip(ends[:-1], ends[1:])
+    )
+    return (
+        output,
+        input_grad,
+        small[0],
+        small[1],
+        small[2],
+        small[3],
+        grad_qkv,
+        small[5, :qkv_columns],
+        grad_dense,
+        small[6],
+        grad_fc1,
+        small[4, :hidden],
+        grad_fc2,
+        small[6],
+    )
+
+
+def fits(mesh):
+    return mesh.shape["dp"] == 8 and mesh.shape["tensor"] == 4
 
 
 def normalize(x_float, gain_row, shift_row):
@@ -293,5 +937,5 @@
         P(),
     )
     return jax.shard_map(
-        on_device, mesh=mesh, in_specs=in_specs, out_specs=out_specs, check_vma=False
-    )
+        fused if fits(mesh) else on_device, mesh=mesh, in_specs=in_specs, out_specs=out_specs, check_vma=False
+    )

time: 683 us -> 350 us (0.51)
  Pallas kernels: 0 us -> 317 us
  waiting for transfers between devices: 277 us -> 0 us
  matrix products: 173 us -> 0 us
  blocking collectives: 85.9 us -> 0 us
  other arithmetic: 75 us -> 14.9 us
  local copies, waits for them, and re-layouts: 47.2 us -> 10.9 us
  between operations: 16.7 us -> 0.94 us
    pallas_call x0 -> x1, Pallas kernels: none -> 317 us  [layer_call(): pl.pallas_call(partial(layer_kernel, jobs=jobs, orders=orders, heads=head...]
    psum x1 -> x0, waiting for transfers between devices: 195 us -> none  [on_device(): full_sum = lax.psum(partial_out, 'tensor')]
    dot_general x24 -> x0, matrix products: 173 us -> none  [the longest x1 33.9 us: on_device(): jnp.einsum('te,ef->tf', cotangent, fc2_weight, preferred_element_type=jnp...]
    psum x2 -> x0, blocking collectives: 85.9 us -> none  [the longest x1 45.7 us: on_device(): lax.psum((gain_grad_one, shift_grad_one, gain_grad_two, shift_grad_two),...]
    reduce_scatter x4 -> x0, waiting for transfers between devices: 82.4 us -> none  [the longest x1 82.4 us: on_device(): lax.psum_scatter(grad_fc2.astype(jnp.bfloat16), 'dp', scatter_dimension=0...]
    convert_element_type x14 -> x0, other arithmetic: 25.4 us -> none  [the longest x1 10 us: on_device(): activated = exact_gelu(hidden).astype(jnp.bfloat16)]
    reduce_sum x7 -> x0, other arithmetic: 24.5 us -> none  [the longest x1 9.25 us: on_device(): out_bias_grad = jnp.sum(out_grad, 0)]
    another operation x6 -> x0, other arithmetic: 13.4 us -> none  [the longest x3 9.03 us: on_device(): jnp.stack([query_pre, key_pre, value_pre], 3)]
  transfers between devices with their start and end apart: 5 -> 0, of which waited for: 2 -> 0; matrix products, arithmetic and copies ran while one was open for 33% -> 0% of each run, Pallas kernels for 0% -> 0%
where the time goes in v1:
time: 350 us; the launch traced here: 344 us
  Pallas kernels  317 us (91%)
  other arithmetic  14.9 us (4%)
  local copies, waits for them, and re-layouts  10.9 us (3%)
    pallas_call x1, Pallas kernels, layer_call(): pl.pallas_call(partial(layer_kernel, jobs=jobs, orders=orders, heads=head...  317 us
    add x3, other arithmetic, fused(): kept[:, a:b].astype(f32) + last[:, a:b].astype(f32)  9.11 us
    unnamed x19, local copies, waits for them, and re-layouts  7.54 us

profile of v1, /device:TPU:0, one launch (start us, length us, event | category | flops | bytes accessed | tf_op | source)
XLA Modules:
  0.0 344.1 jit_solution(4548600592817211756)
XLA Ops:
  0.7 0.1 pad_maximum_fusion
  0.8 0.2 multiply_sine_fusion
  1.0 0.7 constant_dynamic-update-slice_fusion
  1.7 0.7 convert_dynamic-update-slice_fusion.5
  2.4 0.7 convert_dynamic-update-slice_fusion.4
  3.0 0.7 convert_dynamic-update-slice_fusion.3
  3.7 0.7 convert_dynamic-update-slice_fusion
  4.4 0.7 add_dynamic-update-slice_fusion
  5.1 0.7 convert_dynamic-update-slice_fusion.1
  5.8 0.7 convert_dynamic-update-slice_fusion.2
  6.5 0.0 copy-start.5
  6.6 0.6 copy-done.5
  7.1 0.0 copy-start.4
  7.1 0.6 copy-done.4
  7.8 317.4 %layer.1 = (bf16[1024,2048]{1,0:T(8,128)(2,1)}, bf16[1024,2048]{1,0:T(8,128)(2,1)}, bf16[256,6144]{1,0:T(8,128)(2,1)}, bf16[256,6144]{1,0:T(8,128)(2,1)}, f32[8,...) custom-call(bf16[1024,2048]{1,0:T(8,128)(2,1)} %x_hbm.1, ...), custom_call_target="tpu_custom_call" | custom-call | flops 77309411328 | bytes 134217728 | tf_op jit(solution)/shard_map/layer/pallas_call | solution.py:597
  325.2 0.0 copy-start.2
  325.2 1.6 slice_reduce_fusion
  326.8 1.7 fusion.3
  328.5 0.0 copy-start.3
  328.5 1.9 convert_add_fusion.3
  330.4 2.7 convert_add_fusion.2
  333.1 0.0 copy-done.2
  333.1 0.0 copy-start.1
  333.1 4.5 %convert_add_fusion = (f32[256,2048]{1,0:T(8,128)}, f32[256,2048]{1,0:T(8,128)}) fusion(bf16[256,6144]{1,0:T(8,128)(2,1)} %get-tuple-element.23, bf16[256,6144]{1,0:T(8,128)(2,1)S(1)} %copy-done.2), kind=kLoop, calls=%fused_computation | loop fusion | flops 3145728 | bytes 8388608 | tf_op jit(solution)/shard_map/add | solution.py:638
  337.6 0.0 copy-done.3
  337.6 0.6 copy.43
  338.2 0.0 copy-done.1
  338.2 0.0 copy-start
  338.2 2.1 copy.44
  340.3 1.6 copy-done
  341.9 2.0 copy.45
  (10 shorter events, 0.1 us)
Async XLA Ops:
  6.5 0.6 copy-start.5
  7.1 0.6 copy-start.4
  325.2 8.0 %copy-start.2 = (bf16[256,6144]{1,0:T(8,128)(2,1)S(1)}, bf16[256,6144]{1,0:T(8,128)(2,1)}, u32[]{:S(2)}) copy-start(bf16[256,6144]{1,0:T(8,128)(2,1)} %get-tuple-element.22) | copy-start | bytes 9437188
  328.5 9.1 %copy-start.3 = (f32[1,2048]{1,0:T(1,128)}, f32[1,2048]{1,0:T(1,128)S(1)}, u32[]{:S(2)}) copy-start(f32[1,2048]{1,0:T(1,128)S(1)} %get-tuple-element.27) | copy-start | bytes 24580
  333.1 5.1 %copy-start.1 = (bf16[1024,2048]{1,0:T(8,128)(2,1)S(1)}, bf16[1024,2048]{1,0:T(8,128)(2,1)}, u32[]{:S(2)}) copy-start(bf16[1024,2048]{1,0:T(8,128)(2,1)} %get-tuple-element.76) | copy-start | bytes 12582916
  338.2 3.7 %copy-start = (bf16[1024,2048]{1,0:T(8,128)(2,1)S(1)}, bf16[1024,2048]{1,0:T(8,128)(2,1)}, u32[]{:S(2)}) copy-start(bf16[1024,2048]{1,0:T(8,128)(2,1)} %get-tuple-element.77) | copy-start | bytes 12582916
